TPU v7x, 512 devices: a whole 4x4x16 slice. The times are simulated.
512 devices in a mesh: spec: 64 (over x_hi, z, core), img: 8 (over x_lo, y).
Axes of the slice: x: 4 (x_hi: 2, x_lo: 2; x = x_hi * 2 + x_lo), y: 4, z: 16, core: 2. Of those that a mesh axis runs over, the one named last changes fastest.
Arguments:
- spec_emb: bfloat16 [8192, 1024], P('spec', 'img'), may hold values from -1024 to 1024
- img_emb: bfloat16 [2048, 1024], P('img', 'spec'), may hold values from -16 to 16
- grad_spec: bfloat16 [8192, 1024], P('spec', 'img'), may hold values from -6 to 6
- grad_img: bfloat16 [2048, 1024], P('img', 'spec'), may hold values from -6 to 6
Outputs:
- spec_emb_grad: bfloat16 [8192, 1024], P('spec', 'img')
- img_emb_grad: bfloat16 [2048, 1024], P('img', 'spec')
All inputs are finite; a program needn't handle non-finite values.
Results may differ from a plain program's by a relative error of at most 0.0109.
Values may be sent and summed in bfloat16 or wider, within the bound.
No kernel may reach another device: no remote copies, remote signals or barrier semaphores. Data moves between devices by JAX's collectives and lax.ppermute only.
A program may use at most 64 MiB of HBM per device.

v0:
```python
import jax
import jax.numpy as jnp
from jax import lax
from jax.sharding import Mesh
from jax.sharding import PartitionSpec as P

D = 1024
HEADS = 16
SPEC = ("spec_0", "spec_1", "spec_2")


def collected_together(value, axis):
    leaves = jax.tree.leaves(value)
    order = sorted(range(len(leaves)), key=lambda k: -leaves[k].size)
    width = (1, *leaves[order[0]].shape)[-1]
    lines = [
        jnp.pad(leaves[k].reshape(-1), (0, -leaves[k].size % width)).reshape(-1, width)
        for k in order
    ]
    both, at, found = (lax.all_gather(jnp.concatenate(lines), axis), 0, {})
    for k, line in zip(order, lines):
        piece = both[:, at : at + len(line)].reshape(len(both), -1)
        found[k] = piece[:, : leaves[k].size].reshape(-1, *leaves[k].shape)
        at += len(line)
    numbers = iter(range(len(leaves)))
    return jax.tree.map(lambda _: found[next(numbers)], value)


def combined_by_axis(value, axes, combine):
    for axis in axes:
        pieces = collected_together(value, axis)
        value = jax.tree.map(lambda part: part[0], pieces)
        for k in range(1, lax.axis_size(axis)):
            value = combine(value, jax.tree.map(lambda part: part[k], pieces))
    return value


def turned_gather(arrays, axis, dims):
    turned = [jnp.moveaxis(a, dim, 0) for a, dim in zip(arrays, dims)]
    both = jnp.concatenate([t.reshape(len(t), -1) for t in turned], axis=1)
    whole, at, done = (lax.all_gather(both, axis, axis=0, tiled=True), 0, [])
    for t, dim in zip(turned, dims):
        piece = whole[:, at : at + t[0].size].reshape(-1, *t.shape[1:])
        done.append(jnp.moveaxis(piece, 0, dim))
        at += t[0].size
    return tuple(done)


def in_blocks(value, dim, peers):
    before, after = (value.shape[:dim], value.shape[dim + 1 :])
    return jnp.moveaxis(value.reshape(*before, peers, -1, *after), dim, 0)


def summed_on_arrival(value, axis, dim):
    peers = lax.axis_size(axis)
    pieces = lax.all_to_all(in_blocks(value, dim, peers), axis, 0, 0, tiled=True)
    return jnp.sum(pieces, axis=0)


def pair_combine(left_part, right_part):
    highest = jnp.maximum(left_part[0], right_part[0])
    left_factor = jnp.exp(left_part[0] - highest)
    right_factor = jnp.exp(right_part[0] - highest)
    return (
        highest,
        left_part[1] * left_factor + right_part[1] * right_factor,
        left_part[2] * left_factor + right_part[2] * right_factor,
    )


def local_moments(scores, moment, dim):
    highest = jnp.max(scores, axis=dim, keepdims=True)
    scaled = jnp.exp(scores - highest)
    return (
        highest,
        jnp.sum(scaled, axis=dim, keepdims=True),
        jnp.sum(scaled * moment, axis=dim, keepdims=True),
    )


def column_totals(scores, moment):
    highest, total, weighted = combined_by_axis(
        local_moments(scores, moment, 1), SPEC, pair_combine
    )
    weights = jnp.exp(scores - highest) / total
    delta = weighted / total
    return (weights, delta)


def local_row_totals(scores, moment):
    scaled = jnp.exp(scores - jnp.max(scores, axis=2, keepdims=True))
    weights = scaled / jnp.sum(scaled, axis=2, keepdims=True)
    return (weights, jnp.sum(weights * moment, axis=2, keepdims=True))


def score_block(spec_rows, spec_grad, image_rows, image_grad, row_rule, column_rule):
    scale = (D // HEADS) ** (-0.5)
    scores = (
        jnp.einsum("shd,ihd->hsi", spec_rows, image_rows, preferred_element_type=jnp.float32)
        * scale
    )
    row_moment = jnp.einsum(
        "shd,ihd->hsi", spec_grad, image_rows, preferred_element_type=jnp.float32
    )
    column_moment = jnp.einsum(
        "shd,ihd->hsi", spec_rows, image_grad, preferred_element_type=jnp.float32
    )
    row_weight, row_delta = row_rule(scores, row_moment)
    column_weight, column_delta = column_rule(scores, column_moment)
    slope = (
        row_weight * (row_moment - row_delta) + column_weight * (column_moment - column_delta)
    ).astype(jnp.bfloat16)
    spec_part = scale * jnp.einsum(
        "hsi,ihd->shd", slope, image_rows, preferred_element_type=jnp.float32
    )
    spec_part = spec_part + jnp.einsum(
        "hsi,ihd->shd",
        column_weight.astype(jnp.bfloat16),
        image_grad,
        preferred_element_type=jnp.float32,
    )
    image_part = scale * jnp.einsum(
        "hsi,shd->ihd", slope, spec_rows, preferred_element_type=jnp.float32
    )
    image_part = image_part + jnp.einsum(
        "hsi,shd->ihd",
        row_weight.astype(jnp.bfloat16),
        spec_grad,
        preferred_element_type=jnp.float32,
    )
    return (spec_part, image_part)


def shards(spec_emb, img_emb, grad_spec, grad_img):
    head_size = D // HEADS
    spec_count = spec_emb.shape[0]
    image_all, image_grad_all = turned_gather((img_emb, grad_img), SPEC, (1, 1))
    image_local, image_grad_local = (
        lax.all_to_all(image_all, "img", split_axis=1, concat_axis=0, tiled=True),
        lax.all_to_all(image_grad_all, "img", split_axis=1, concat_axis=0, tiled=True),
    )
    local_width = spec_emb.shape[1]
    local_heads = local_width // head_size
    image_count = image_local.shape[0]
    spec_heads = spec_emb.reshape(spec_count, local_heads, head_size)
    spec_grad_heads = grad_spec.reshape(spec_count, local_heads, head_size)
    image_heads = image_local.reshape(image_count, local_heads, head_size)
    image_grad_heads = image_grad_local.reshape(image_count, local_heads, head_size)
    spec_parts = []
    image_parts = []
    for head_index in range(local_heads):
        window = slice(head_index, head_index + 1)
        spec_part, image_part = score_block(
            spec_heads[:, window],
            spec_grad_heads[:, window],
            image_heads[:, window],
            image_grad_heads[:, window],
            local_row_totals,
            column_totals,
        )
        spec_parts.append(spec_part)
        image_parts.append(image_part)
    spec_result = (
        jnp.concatenate(spec_parts, axis=1).reshape(spec_count, local_width).astype(jnp.bfloat16)
    )
    image_total = jnp.concatenate(image_parts, axis=1).reshape(image_count, local_width)
    image_back = lax.all_to_all(image_total, "img", split_axis=0, concat_axis=1, tiled=True)
    image_result = summed_on_arrival(image_back, SPEC, 1).astype(jnp.bfloat16)
    return (spec_result, image_result)


def solution(mesh):
    split = Mesh(
        mesh.devices.reshape(2, 16, 2, mesh.shape["img"]), ("spec_0", "spec_1", "spec_2", "img")
    )
    return jax.shard_map(
        shards,
        mesh=split,
        in_specs=(P(SPEC, "img"), P("img", SPEC), P(SPEC, "img"), P("img", SPEC)),
        out_specs=(P(SPEC, "img"), P("img", SPEC)),
        check_vma=False,
    )
```

profile of v0, /device:TPU:33, one launch (start us, length us, event | category | flops | bytes accessed | tf_op | source)
XLA Modules:
  0.0 371.6 jit_solution(16061481993177456034)
XLA Ops:
  7.2 0.0 all-gather.14.cloned.1.call-start
  7.2 1.3 pad_maximum_fusion.2
  8.5 0.0 all-gather.14.cloned.1.call-update
  8.6 148.4 %all-gather.14.cloned.1.call-done = bf16[1024,512]{1,0:T(8,128)(2,1)} async-done(((bf16[16,512]{1,0:T(8,128)(2,1)}), bf16[1024,512]{1,0:T(8,128)(2,1)}) %all-gather.14.cloned.1.call-update) | async-done | bytes 1048592 | tf_op jit(solution)/shard_map/all_gather | solution.py:41
  157.0 2.3 fusion.160
  159.3 4.1 %all-to-all-start = ((bf16[256,8,128]{0,2,1:T(8,128)(2,1)}), bf16[256,8,128]{0,2,1:T(8,128)(2,1)S(1)}, u32[]{:S(2)}, u32[]{:S(2)}) async-start(bf16[256,8,128]{0,2,1:T(8,128)(2,1)} %bitcast.3), calls=%async_computation | async-start | bytes 1048576 | tf_op jit(solution)/shard_map/all_to_all | solution.py:139
  163.4 0.0 copy-done.5
  163.4 0.0 copy-start.6
  163.5 0.1 copy.22
  163.6 0.6 copy-done.6
  164.2 0.1 copy.23
  164.3 7.4 %all-to-all-done = bf16[256,8,128]{0,2,1:T(8,128)(2,1)S(1)} async-done(((bf16[256,8,128]{0,2,1:T(8,128)(2,1)}), bf16[256,8,128]{0,2,1:T(8,128)(2,1)S(1)}, u32[]{:S(2)}, u32[]{:S(2)}) %all-to-all-start) | async-done | bytes 524320 | tf_op jit(solution)/shard_map/all_to_all | solution.py:139
  171.7 4.7 %all-to-all-start.1 = ((bf16[256,8,128]{0,2,1:T(8,128)(2,1)}), bf16[256,8,128]{0,2,1:T(8,128)(2,1)S(1)}, u32[]{:S(2)}, u32[]{:S(2)}) async-start(bf16[256,8,128]{0,2,1:T(8,128)(2,1)} %bitcast.15), calls=%async_computation.1 | async-start | bytes 1048576 | tf_op jit(solution)/shard_map/all_to_all | solution.py:140
  176.4 0.3 copy.21
  176.7 0.2 reshape.515
  177.0 0.6 fusion.157
  177.6 0.6 fusion.156
  178.2 6.3 %all-to-all-done.1 = bf16[256,8,128]{0,2,1:T(8,128)(2,1)S(1)} async-done(((bf16[256,8,128]{0,2,1:T(8,128)(2,1)}), bf16[256,8,128]{0,2,1:T(8,128)(2,1)S(1)}, u32[]{:S(2)}, u32[]{:S(2)}) %all-to-all-start.1) | async-done | bytes 524320 | tf_op jit(solution)/shard_map/all_to_all | solution.py:140
  184.5 1.1 copy.24
  185.6 1.3 reshape.521
  186.9 0.0 copy-start.2
  186.9 1.1 fusion.12
  187.9 0.0 copy-done.2
  188.0 4.9 %all-gather.6 = f32[2,3,2048]{2,1,0:T(4,128)S(1)} all-gather(f32[1,3,2048]{2,1,0:T(4,128)S(1)} %maximum_bitcast_fusion), channel_id=2, replica_groups=mesh['spec_0'=2,'spec_1'=16,'spec_2'=2,'img'=8] {'spec_0'}, dimensions={0}, use_global_device_ids=true | all-gather | bytes 73728 | tf_op jit(solution)/shard_map/all_gather | solution.py:20
  193.0 22.7 %all-gather.7 = f32[16,3,2048]{2,1,0:T(4,128)S(1)} all-gather(f32[1,3,2048]{2,1,0:T(4,128)S(1)} %maximum_bitcast_fusion.1), channel_id=3, replica_groups=mesh['spec_0'=2,'spec_1'=16,'spec_2'=2,'img'=8] {'spec_1'}, dimensions={0}, use_global_device_ids=true | all-gather | bytes 417792 | tf_op jit(solution)/shard_map/all_gather | solution.py:20
  215.7 0.4 fusion.150
  216.1 0.4 fusion.151
  216.5 12.0 %all-gather.8 = f32[2,3,2048]{2,1,0:T(4,128)S(1)} all-gather(f32[1,3,2048]{2,1,0:T(4,128)S(1)} %maximum_bitcast_fusion.2), channel_id=4, replica_groups=mesh['spec_0'=2,'spec_1'=16,'spec_2'=2,'img'=8] {'spec_2'}, dimensions={0}, use_global_device_ids=true | all-gather | bytes 73728 | tf_op jit(solution)/shard_map/all_gather | solution.py:20
  228.5 0.1 fusion.84
  228.6 0.5 fusion.9
  229.1 1.5 fusion.8
  230.6 0.3 convolution_multiply_fusion.3
  230.9 0.0 copy-start.3
  230.9 0.3 fusion
  231.2 0.7 copy-done.3
  231.9 1.1 fusion.15
  233.0 4.9 %all-gather.9 = f32[2,3,2048]{2,1,0:T(4,128)S(1)} all-gather(f32[1,3,2048]{2,1,0:T(4,128)S(1)} %maximum_bitcast_fusion.3), channel_id=5, replica_groups=mesh['spec_0'=2,'spec_1'=16,'spec_2'=2,'img'=8] {'spec_0'}, dimensions={0}, use_global_device_ids=true | all-gather | bytes 73728 | tf_op jit(solution)/shard_map/all_gather | solution.py:20
  238.1 23.8 %all-gather.10 = f32[16,3,2048]{2,1,0:T(4,128)S(1)} all-gather(f32[1,3,2048]{2,1,0:T(4,128)S(1)} %maximum_bitcast_fusion.4), channel_id=6, replica_groups=mesh['spec_0'=2,'spec_1'=16,'spec_2'=2,'img'=8] {'spec_1'}, dimensions={0}, use_global_device_ids=true | all-gather | bytes 417792 | tf_op jit(solution)/shard_map/all_gather | solution.py:20
  261.8 0.4 fusion.152
  262.2 0.4 fusion.153
  262.7 9.8 %all-gather.11 = f32[2,3,2048]{2,1,0:T(4,128)S(1)} all-gather(f32[1,3,2048]{2,1,0:T(4,128)S(1)} %maximum_bitcast_fusion.5), channel_id=7, replica_groups=mesh['spec_0'=2,'spec_1'=16,'spec_2'=2,'img'=8] {'spec_2'}, dimensions={0}, use_global_device_ids=true | all-gather | bytes 73728 | tf_op jit(solution)/shard_map/all_gather | solution.py:20
  272.4 0.1 fusion.21
  272.5 0.5 fusion.7
  273.0 1.5 fusion.6
  274.5 0.0 copy-start
  274.5 0.3 convolution_multiply_fusion.2
  274.8 0.5 copy-done
  275.3 0.3 fusion.1
  275.6 0.1 pad_maximum_fusion
  275.7 0.3 copy.33
  276.0 0.3 copy.29
  276.4 17.6 %all_to_all.53 = f32[8,256,128]{1,2,0:T(8,128)} all-to-all(f32[8,256,128]{1,2,0:T(8,128)S(1)} %copy.29), channel_id=1, replica_groups=mesh['spec_0'=2,'spec_1'=16,'spec_2'=2,'img'=8] {'img'}, dimensions={0} | all-to-all | bytes 2097152 | tf_op jit(solution)/shard_map/all_to_all | solution.py:167
  294.0 13.2 %all-to-all-start.3 = ((f32[64,256,16]{1,2,0:T(8,128)}), f32[64,256,16]{1,2,0:T(8,128)}, u32[]{:S(2)}, u32[]{:S(2)}) async-start(f32[64,256,16]{1,2,0:T(8,128)} %bitcast.185), calls=%async_computation.3 | async-start | bytes 2097152 | tf_op jit(solution)/shard_map/all_to_all | solution.py:56
  307.1 0.0 copy-start.1
  307.2 0.2 convolution_multiply_fusion.5
  307.4 0.8 copy-done.1
  308.2 0.0 copy-start.4
  308.2 0.2 convolution_multiply_fusion.4
  308.4 0.8 copy-done.4
  309.2 0.8 fusion.5
  310.0 0.8 fusion.4
  310.8 0.7 copy.30
  311.5 51.3 %all-to-all-done.3 = f32[64,256,16]{1,2,0:T(8,128)} async-done(((f32[64,256,16]{1,2,0:T(8,128)}), f32[64,256,16]{1,2,0:T(8,128)}, u32[]{:S(2)}, u32[]{:S(2)}) %all-to-all-start.3) | async-done | bytes 1048608 | tf_op jit(solution)/shard_map/all_to_all | solution.py:56
  362.8 1.9 reduce_sum.101
  (12 shorter events, 0.3 us)
Async XLA Ops:
  7.2 149.8 %all-gather.14.cloned.1.call-start = ((), (), s32[]{:S(2)}) async-start(), calls=%async_computation.4 | async-start | bytes 1064960 | tf_op jit(solution)/shard_map/all_gather | solution.py:41
  159.3 4.2 %copy-start.5 = (bf16[128,128]{1,0:T(8,128)(2,1)S(1)}, bf16[128,128]{1,0:T(8,128)(2,1)}, u32[]{:S(2)}) copy-start(bf16[128,128]{1,0:T(8,128)(2,1)} %param.4) | copy-start | bytes 98308
  159.3 12.4 %all-to-all-start = ((bf16[256,8,128]{0,2,1:T(8,128)(2,1)}), bf16[256,8,128]{0,2,1:T(8,128)(2,1)S(1)}, u32[]{:S(2)}, u32[]{:S(2)}) async-start(bf16[256,8,128]{0,2,1:T(8,128)(2,1)} %bitcast.3), calls=%async_computation | async-start | bytes 1048576 | tf_op jit(solution)/shard_map/all_to_all | solution.py:139
  163.4 0.8 copy-start.6
  171.7 12.7 %all-to-all-start.1 = ((bf16[256,8,128]{0,2,1:T(8,128)(2,1)}), bf16[256,8,128]{0,2,1:T(8,128)(2,1)S(1)}, u32[]{:S(2)}, u32[]{:S(2)}) async-start(bf16[256,8,128]{0,2,1:T(8,128)(2,1)} %bitcast.15), calls=%async_computation.1 | async-start | bytes 1048576 | tf_op jit(solution)/shard_map/all_to_all | solution.py:140
  186.9 1.1 copy-start.2
  230.9 1.0 copy-start.3
  274.5 0.8 copy-start
  294.0 68.8 %all-to-all-start.3 = ((f32[64,256,16]{1,2,0:T(8,128)}), f32[64,256,16]{1,2,0:T(8,128)}, u32[]{:S(2)}, u32[]{:S(2)}) async-start(f32[64,256,16]{1,2,0:T(8,128)} %bitcast.185), calls=%async_computation.3 | async-start | bytes 2097152 | tf_op jit(solution)/shard_map/all_to_all | solution.py:56
  307.1 1.0 copy-start.1
  308.2 1.0 copy-start.4
Sparse Core Ops, SparseCore 0:
  11.8 145.1 all-gather.13
where the time goes:
time: 372 us
  waiting for transfers between devices  214 us (58%)
  blocking collectives  95.7 us (26%)
  starting transfers between devices  22.1 us (6%)
  between operations  14.3 us (4%)
  local copies, waits for them, and re-layouts  10.3 us (3%)
  other arithmetic  8.32 us (2%)
  matrix products  7.43 us (2%)
    all_gather x1, waiting for transfers between devices, turned_gather(): whole, at, done = (lax.all_gather(both, axis, axis=0, tiled=True), 0, [])  148 us
    all_gather x6, blocking collectives, collected_together(): both, at, found = (lax.all_gather(jnp.concatenate(lines), axis), 0, {})  78.1 us
    all_to_all x1, waiting for transfers between devices, summed_on_arrival(): lax.all_to_all(in_blocks(value, dim, peers), axis, 0, 0, tiled=True)  51.3 us
    all_to_all x1, blocking collectives, shards(): lax.all_to_all(image_total, 'img', split_axis=0, concat_axis=1, tiled=True)  17.6 us
    all_to_all x1, starting transfers between devices, summed_on_arrival(): lax.all_to_all(in_blocks(value, dim, peers), axis, 0, 0, tiled=True)  13.2 us
  transfers between devices with their start and end apart: 4, of which 4 were waited for; matrix products, arithmetic and copies ran while one was open for 1% of the time, Pallas kernels for 0%

commit v1 on v0

--- a/solution.py
+++ b/solution.py
@@ -7,6 +7,13 @@
 D = 1024
 HEADS = 16
 SPEC = ("spec_0", "spec_1", "spec_2")
+
+
+def all_by_exchange(x, mesh_axis, dim):
+    devices = lax.axis_size(mesh_axis)
+    pieces = jnp.stack([x for _ in range(devices)])
+    pieces = lax.all_to_all(pieces, mesh_axis, split_axis=0, concat_axis=0)
+    return jnp.concatenate(pieces, axis=dim)
 
 
 def collected_together(value, axis):
@@ -38,7 +45,7 @@
 def turned_gather(arrays, axis, dims):
     turned = [jnp.moveaxis(a, dim, 0) for a, dim in zip(arrays, dims)]
     both = jnp.concatenate([t.reshape(len(t), -1) for t in turned], axis=1)
-    whole, at, done = (lax.all_gather(both, axis, axis=0, tiled=True), 0, [])
+    whole, at, done = (all_by_exchange(both, axis, 0), 0, [])
     for t, dim in zip(turned, dims):
         piece = whole[:, at : at + t[0].size].reshape(-1, *t.shape[1:])
         done.append(jnp.moveaxis(piece, 0, dim))

time: 372 us -> 279 us (0.75)
  waiting for transfers between devices: 214 us -> 64.2 us
  blocking collectives: 95.7 us -> 170 us
  between operations: 14.3 us -> 0.9 us
    all_gather x1 -> x0, waiting for transfers between devices: 148 us -> none  [turned_gather(): whole, at, done = (lax.all_gather(both, axis, axis=0, tiled=True), 0, [])]
    all_to_all x0 -> x1, blocking collectives: none -> 74 us  [all_by_exchange(): pieces = lax.all_to_all(pieces, mesh_axis, split_axis=0, concat_axis=0)]
  transfers between devices with their start and end apart: 4 -> 3, of which waited for: 4 -> 3; matrix products, arithmetic and copies ran while one was open for 1% -> 2% of each run, Pallas kernels for 0% -> 0%
where the time goes in v1:
time: 279 us; the launch traced here: 278 us
  blocking collectives  170 us (61%)
  waiting for transfers between devices  64.2 us (23%)
  starting transfers between devices  18.7 us (7%)
  local copies, waits for them, and re-layouts  9.16 us (3%)
  other arithmetic  7.71 us (3%)
  matrix products  7.43 us (3%)
    all_gather x6, blocking collectives, collected_together(): both, at, found = (lax.all_gather(jnp.concatenate(lines), axis), 0, {})  78.1 us
    all_to_all x1, blocking collectives, all_by_exchange(): pieces = lax.all_to_all(pieces, mesh_axis, split_axis=0, concat_axis=0)  74 us
    all_to_all x1, waiting for transfers between devices, summed_on_arrival(): lax.all_to_all(in_blocks(value, dim, peers), axis, 0, 0, tiled=True)  51.3 us
    all_to_all x1, blocking collectives, shards(): lax.all_to_all(image_total, 'img', split_axis=0, concat_axis=1, tiled=True)  17.6 us
    all_to_all x1, starting transfers between devices, summed_on_arrival(): lax.all_to_all(in_blocks(value, dim, peers), axis, 0, 0, tiled=True)  10.9 us
    all_to_all x1, waiting for transfers between devices, shards(): lax.all_to_all(image_grad_all, 'img', split_axis=1, concat_axis=0, tiled=...  6.61 us
    all_to_all x1, waiting for transfers between devices, shards(): lax.all_to_all(image_all, 'img', split_axis=1, concat_axis=0, tiled=True)  6.3 us
  transfers between devices with their start and end apart: 3, of which 3 were waited for; matrix products, arithmetic and copies ran while one was open for 2% of the time, Pallas kernels for 0%

profile of v1, /device:TPU:33, one launch (start us, length us, event | category | flops | bytes accessed | tf_op | source)
XLA Modules:
  0.0 277.9 jit_solution(12040828502538205042)
XLA Ops:
  0.6 0.7 pad_maximum_fusion.2
  1.3 0.1 stack.2
  1.5 74.0 %all_to_all.58 = bf16[64,16,512]{2,1,0:T(8,128)(2,1)S(1)} all-to-all(bf16[64,16,512]{2,1,0:T(8,128)(2,1)S(1)} %stack.2), channel_id=1, replica_groups=mesh['spec_0'=2,'spec_1'=16,'spec_2'=2,'img'=8] {'spec_0','spec_1','spec..., dimensions={0} | all-to-all | bytes 2097152 | tf_op jit(solution)/shard_map/all_to_all | solution.py:15
  75.5 1.1 fusion.160
  76.6 0.0 copy-start.5
  76.6 4.4 %all-to-all-start.1 = ((bf16[256,8,128]{0,2,1:T(8,128)(2,1)}), bf16[256,8,128]{0,2,1:T(8,128)(2,1)S(1)}, u32[]{:S(2)}, u32[]{:S(2)}) async-start(bf16[256,8,128]{0,2,1:T(8,128)(2,1)} %bitcast.4), calls=%async_computation.1 | async-start | bytes 1048576 | tf_op jit(solution)/shard_map/all_to_all | solution.py:146
  80.9 0.0 copy-done.5
  80.9 0.0 copy-start.6
  80.9 0.1 copy.30
  81.0 0.6 copy-done.6
  81.7 0.1 copy.31
  81.8 6.3 %all-to-all-done.1 = bf16[256,8,128]{0,2,1:T(8,128)(2,1)S(1)} async-done(((bf16[256,8,128]{0,2,1:T(8,128)(2,1)}), bf16[256,8,128]{0,2,1:T(8,128)(2,1)S(1)}, u32[]{:S(2)}, u32[]{:S(2)}) %all-to-all-start.1) | async-done | bytes 524320 | tf_op jit(solution)/shard_map/all_to_all | solution.py:146
  88.1 3.5 %all-to-all-start.2 = ((bf16[256,8,128]{0,2,1:T(8,128)(2,1)}), bf16[256,8,128]{0,2,1:T(8,128)(2,1)S(1)}, u32[]{:S(2)}, u32[]{:S(2)}) async-start(bf16[256,8,128]{0,2,1:T(8,128)(2,1)} %bitcast.16), calls=%async_computation.2 | async-start | bytes 1048576 | tf_op jit(solution)/shard_map/all_to_all | solution.py:147
  91.6 0.3 copy.29
  91.9 0.2 reshape.521
  92.1 0.6 fusion.157
  92.7 0.6 fusion.156
  93.3 6.6 %all-to-all-done.2 = bf16[256,8,128]{0,2,1:T(8,128)(2,1)S(1)} async-done(((bf16[256,8,128]{0,2,1:T(8,128)(2,1)}), bf16[256,8,128]{0,2,1:T(8,128)(2,1)S(1)}, u32[]{:S(2)}, u32[]{:S(2)}) %all-to-all-start.2) | async-done | bytes 524320 | tf_op jit(solution)/shard_map/all_to_all | solution.py:147
  99.9 1.1 copy.32
  101.0 1.3 reshape.527
  102.3 0.0 copy-start.2
  102.3 1.1 fusion.12
  103.4 0.0 copy-done.2
  103.4 4.9 %all-gather.6 = f32[2,3,2048]{2,1,0:T(4,128)S(1)} all-gather(f32[1,3,2048]{2,1,0:T(4,128)S(1)} %maximum_bitcast_fusion), channel_id=2, replica_groups=mesh['spec_0'=2,'spec_1'=16,'spec_2'=2,'img'=8] {'spec_0'}, dimensions={0}, use_global_device_ids=true | all-gather | bytes 73728 | tf_op jit(solution)/shard_map/all_gather | solution.py:27
  108.5 23.2 %all-gather.7 = f32[16,3,2048]{2,1,0:T(4,128)S(1)} all-gather(f32[1,3,2048]{2,1,0:T(4,128)S(1)} %maximum_bitcast_fusion.1), channel_id=3, replica_groups=mesh['spec_0'=2,'spec_1'=16,'spec_2'=2,'img'=8] {'spec_1'}, dimensions={0}, use_global_device_ids=true | all-gather | bytes 417792 | tf_op jit(solution)/shard_map/all_gather | solution.py:27
  131.7 0.4 fusion.150
  132.1 0.4 fusion.151
  132.5 12.5 %all-gather.8 = f32[2,3,2048]{2,1,0:T(4,128)S(1)} all-gather(f32[1,3,2048]{2,1,0:T(4,128)S(1)} %maximum_bitcast_fusion.2), channel_id=4, replica_groups=mesh['spec_0'=2,'spec_1'=16,'spec_2'=2,'img'=8] {'spec_2'}, dimensions={0}, use_global_device_ids=true | all-gather | bytes 73728 | tf_op jit(solution)/shard_map/all_gather | solution.py:27
  145.0 0.1 fusion.84
  145.0 0.5 fusion.9
  145.5 1.5 fusion.8
  147.0 0.3 convolution_multiply_fusion.3
  147.3 0.0 copy-start.3
  147.3 0.3 fusion
  147.7 0.7 copy-done.3
  148.4 1.1 fusion.15
  149.4 4.9 %all-gather.9 = f32[2,3,2048]{2,1,0:T(4,128)S(1)} all-gather(f32[1,3,2048]{2,1,0:T(4,128)S(1)} %maximum_bitcast_fusion.3), channel_id=5, replica_groups=mesh['spec_0'=2,'spec_1'=16,'spec_2'=2,'img'=8] {'spec_0'}, dimensions={0}, use_global_device_ids=true | all-gather | bytes 73728 | tf_op jit(solution)/shard_map/all_gather | solution.py:27
  154.5 22.8 %all-gather.10 = f32[16,3,2048]{2,1,0:T(4,128)S(1)} all-gather(f32[1,3,2048]{2,1,0:T(4,128)S(1)} %maximum_bitcast_fusion.4), channel_id=6, replica_groups=mesh['spec_0'=2,'spec_1'=16,'spec_2'=2,'img'=8] {'spec_1'}, dimensions={0}, use_global_device_ids=true | all-gather | bytes 417792 | tf_op jit(solution)/shard_map/all_gather | solution.py:27
  177.3 0.4 fusion.152
  177.7 0.4 fusion.153
  178.1 9.8 %all-gather.11 = f32[2,3,2048]{2,1,0:T(4,128)S(1)} all-gather(f32[1,3,2048]{2,1,0:T(4,128)S(1)} %maximum_bitcast_fusion.5), channel_id=7, replica_groups=mesh['spec_0'=2,'spec_1'=16,'spec_2'=2,'img'=8] {'spec_2'}, dimensions={0}, use_global_device_ids=true | all-gather | bytes 73728 | tf_op jit(solution)/shard_map/all_gather | solution.py:27
  187.9 0.1 fusion.21
  187.9 0.5 fusion.7
  188.4 1.5 fusion.6
  189.9 0.0 copy-start
  189.9 0.3 convolution_multiply_fusion.2
  190.2 0.5 copy-done
  190.7 0.3 fusion.1
  191.0 0.1 pad_maximum_fusion
  191.1 0.3 copy.41
  191.5 0.3 copy.37
  191.8 17.6 %all_to_all.59 = f32[8,256,128]{1,2,0:T(8,128)} all-to-all(f32[8,256,128]{1,2,0:T(8,128)S(1)} %copy.37), channel_id=1, replica_groups=mesh['spec_0'=2,'spec_1'=16,'spec_2'=2,'img'=8] {'img'}, dimensions={0} | all-to-all | bytes 2097152 | tf_op jit(solution)/shard_map/all_to_all | solution.py:174
  209.4 10.9 %all-to-all-start.4 = ((f32[64,256,16]{1,2,0:T(8,128)}), f32[64,256,16]{1,2,0:T(8,128)}, u32[]{:S(2)}, u32[]{:S(2)}) async-start(f32[64,256,16]{1,2,0:T(8,128)} %bitcast.186), calls=%async_computation.4 | async-start | bytes 2097152 | tf_op jit(solution)/shard_map/all_to_all | solution.py:63
  220.3 0.0 copy-start.1
  220.3 0.2 convolution_multiply_fusion.5
  220.6 0.8 copy-done.1
  221.4 0.0 copy-start.4
  221.4 0.2 convolution_multiply_fusion.4
  221.6 0.8 copy-done.4
  222.4 0.8 fusion.5
  223.2 0.8 fusion.4
  223.9 0.7 copy.38
  224.7 51.3 %all-to-all-done.4 = f32[64,256,16]{1,2,0:T(8,128)} async-done(((f32[64,256,16]{1,2,0:T(8,128)}), f32[64,256,16]{1,2,0:T(8,128)}, u32[]{:S(2)}, u32[]{:S(2)}) %all-to-all-start.4) | async-done | bytes 1048608 | tf_op jit(solution)/shard_map/all_to_all | solution.py:63
  276.0 1.9 reduce_sum.101
  (11 shorter events, 0.3 us)
Async XLA Ops:
  76.6 4.4 %copy-start.5 = (bf16[128,128]{1,0:T(8,128)(2,1)S(1)}, bf16[128,128]{1,0:T(8,128)(2,1)}, u32[]{:S(2)}) copy-start(bf16[128,128]{1,0:T(8,128)(2,1)} %param.4) | copy-start | bytes 98308
  76.6 11.5 %all-to-all-start.1 = ((bf16[256,8,128]{0,2,1:T(8,128)(2,1)}), bf16[256,8,128]{0,2,1:T(8,128)(2,1)S(1)}, u32[]{:S(2)}, u32[]{:S(2)}) async-start(bf16[256,8,128]{0,2,1:T(8,128)(2,1)} %bitcast.4), calls=%async_computation.1 | async-start | bytes 1048576 | tf_op jit(solution)/shard_map/all_to_all | solution.py:146
  80.9 0.8 copy-start.6
  88.1 11.8 %all-to-all-start.2 = ((bf16[256,8,128]{0,2,1:T(8,128)(2,1)}), bf16[256,8,128]{0,2,1:T(8,128)(2,1)S(1)}, u32[]{:S(2)}, u32[]{:S(2)}) async-start(bf16[256,8,128]{0,2,1:T(8,128)(2,1)} %bitcast.16), calls=%async_computation.2 | async-start | bytes 1048576 | tf_op jit(solution)/shard_map/all_to_all | solution.py:147
  102.3 1.1 copy-start.2
  147.3 1.0 copy-start.3
  189.9 0.8 copy-start
  209.4 66.6 %all-to-all-start.4 = ((f32[64,256,16]{1,2,0:T(8,128)}), f32[64,256,16]{1,2,0:T(8,128)}, u32[]{:S(2)}, u32[]{:S(2)}) async-start(f32[64,256,16]{1,2,0:T(8,128)} %bitcast.186), calls=%async_computation.4 | async-start | bytes 2097152 | tf_op jit(solution)/shard_map/all_to_all | solution.py:63
  220.3 1.0 copy-start.1
  221.4 1.0 copy-start.4
